TPU v7x, 32 devices: a whole 2x2x4 slice. The times are simulated.
32 devices in a mesh: pts: 8 (over y, x, core), wlk: 4 (over z).
Axes of the slice: x: 2, y: 2, z: 4, core: 2. Of those that a mesh axis runs over, the one named last changes fastest.
Arguments:
- green_half: bfloat16 [8, 400, 2400], P('wlk'), may hold values from -6 to 6
- collocation: bfloat16 [2400, 9600], P('wlk', 'pts'), may hold values from -0.125 to 0.125
- occupied: bfloat16 [9600, 400], P('pts'), may hold values from -0.0029296875 to 0.0029296875
- kernel: bfloat16 [9600, 9600], P('pts'), may hold values from 0 to 16, as said below
Outputs:
- potential: float32 [8, 9600], P('wlk', 'pts')
- coulomb_energy: float32 [8], P('wlk')
- exchange_energy: float32 [8], P('wlk')
Inputs may be any that keep to these rules, and one draw needn't show every extreme that they name: kernel is symmetric and positive definite: kernel[p, q] equals kernel[q, p].
All inputs are finite; a program needn't handle non-finite values.
Results may differ from a plain program's by a relative error of at most 0.008.
Values may be sent and summed in bfloat16 or wider, within the bound.
A program may use at most 192 MiB of HBM per device.

v0:
```python
import jax
import jax.numpy as jnp
from jax import lax
from jax.sharding import PartitionSpec as P


def passed_along(block, axis, distance):
    devices = range(lax.axis_size(axis))
    route = [((i - distance) % len(devices), i) for i in devices]
    return lax.ppermute(block, axis, route)


def local(green_half, collocation, occupied, kernel):
    pts_rows = occupied.shape[0]
    theta = jnp.einsum(
        "mp,wim->pwi",
        lax.all_gather(collocation, "wlk", axis=0, tiled=True),
        green_half,
        preferred_element_type=jnp.float32,
    ).astype(jnp.bfloat16)
    density = jnp.einsum("pwi,pi->wp", theta, occupied, preferred_element_type=jnp.float32)
    density_b = density.astype(jnp.bfloat16)

    def block_terms(start, theta_far, occ_far):
        cross_near = jnp.einsum("awi,bi->wab", theta, occ_far, preferred_element_type=jnp.float32)
        cross_far = jnp.einsum(
            "ai,bwi->wab", occupied, theta_far, preferred_element_type=jnp.float32
        )
        kernel_part = lax.dynamic_slice_in_dim(kernel, start, occ_far.shape[0], 1).astype(
            jnp.float32
        )
        return jnp.sum(kernel_part[None] * cross_near * cross_far, axis=(1, 2))

    density_all = lax.all_gather(density_b, "pts", axis=1, tiled=True)
    potential = jnp.einsum("wq,aq->wa", density_all, kernel, preferred_element_type=jnp.float32)
    devices = lax.axis_size("pts")
    position = lax.axis_index("pts")
    exchange_sum = block_terms(position * pts_rows, theta, occupied)
    travel = (theta, occupied)
    for stride in range(1, devices // 2 + 1):
        travel = passed_along((travel[0], travel[1]), "pts", 1)
        source = (position - stride) % devices
        weight = 1.0 if 2 * stride == devices else 2.0
        exchange_sum = exchange_sum + weight * block_terms(source * pts_rows, travel[0], travel[1])
    coulomb = 0.5 * jnp.sum(density * potential, axis=1)
    coulomb_energy, exchange_energy = lax.psum((coulomb, -0.5 * exchange_sum), "pts")
    return (potential, coulomb_energy, exchange_energy)


def solution(mesh):
    placed = (P("wlk", None, None), P("wlk", "pts"), P("pts", None), P("pts", None))
    return jax.shard_map(
        local,
        mesh=mesh,
        in_specs=placed,
        out_specs=(P("wlk", "pts"), P("wlk"), P("wlk")),
        check_vma=False,
    )
```

profile of v0, /device:TPU:0, one launch (start us, length us, event | category | flops | bytes accessed | tf_op | source)
XLA Modules:
  0.0 310.9 jit_solution(14020435606796289344)
XLA Ops:
  7.2 0.7 all-gather.3.cloned.1.call-update
  8.4 15.3 %collective-permute-done = bf16[1200,400]{0,1:T(8,128)(2,1)S(1)} collective-permute-done((bf16[1200,400]{0,1:T(8,128)(2,1)}, bf16[1200,400]{0,1:T(8,128)(2,1)S(1)}, u32[]{:S(2)}, u32[]{:S(2)}) %collective-permute-start) | collective-permute-done | bytes 960032 | tf_op jit(solution)/shard_map/ppermute | solution.py:10
  23.8 3.1 convert.2
  26.8 11.8 %collective-permute-done.2 = bf16[1200,400]{0,1:T(8,128)(2,1)S(1)} collective-permute-done((bf16[1200,400]{0,1:T(8,128)(2,1)S(1)}, bf16[1200,400]{0,1:T(8,128)(2,1)S(1)}, u32[]{:S(2)}, u32[]{:S(2)}) %collective-permute-start.2) | collective-permute-done | bytes 960032 | tf_op jit(solution)/shard_map/ppermute | solution.py:10
  38.6 86.6 %all-gather.3.cloned.1.call-done = bf16[2400,1200]{1,0:T(8,128)(2,1)} async-done(((bf16[600,1200]{1,0:T(8,128)(2,1)}), bf16[2400,1200]{1,0:T(8,128)(2,1)}) %all-gather.3.cloned.1.call-update) | async-done | bytes 5760016 | tf_op jit(solution)/shard_map/all_gather | solution.py:17
  125.2 9.4 %multiply_reduce_fusion = (f32[1200,2]{0,1:T(2,128)S(1)}, bf16[1200,2,400]{0,2,1:T(8,128)(2,1)S(1)}) fusion(f32[1200,400]{0,1:T(8,128)} %convert.2, bf16[2,400,2400]{2,1,0:T(8,128)(2,1)} %param.4, bf16[2400,1200]{1,0:T(8,128)(2,1)} %all-gather.3.cloned.1.call-done), kind=kOutput, calls=%fused_computation.20 | convolution fusion | flops 4611837440 | bytes 13449600 | tf_op jit(solution)/shard_map/mp,wim->pwi/dot_general | solution.py:15
  134.7 17.5 %dynamic-slice_convert_fusion.3 = (f32[1200,1200]{1,0:T(8,128)}, f32[1200,1200]{1,0:T(8,128)}, f32[1200,1200]{1,0:T(8,128)}, f32[1200,1200]{1,0:T(8,128)}, f32[1200,1200]{1,0:T(8,128)}) fusion(bf16[1200,9600]{1,0:T(8,128)(2,1)} %param.7, s32[]{:T(128)S(6)} %select_n.36, s32[]{:T(128)S(6)} %select_n.38, s32[]{:T(128)S(6)} %select_n.34, s32[]{:T(128)S(6)} %select_n.42, ...), kind=kLoop, calls=%fused_computation.25 | loop fusion | flops 7200000 | bytes 43200020 | tf_op jit(solution)/shard_map/convert_element_type | solution.py:29
  152.1 7.8 %copy.21 = f32[1200,1200]{0,1:T(8,128)} copy(f32[1200,1200]{1,0:T(8,128)} %get-tuple-element.7) | data formatting | bytes 11520000 | tf_op jit(solution)/shard_map/convert_element_type | solution.py:29
  160.0 1.5 collective-permute-start.6
  161.5 16.0 %all-gather = bf16[8,1200,2]{1,2,0:T(2,128)(2,1)S(1)} all-gather(bf16[1,1200,2]{1,2,0:T(2,128)(2,1)S(1)} %fusion.29), channel_id=1, replica_groups=mesh['pts'=8,'wlk'=4] {'pts'}, dimensions={0}, use_global_device_ids=true | all-gather | bytes 43200 | tf_op jit(solution)/shard_map/all_gather | solution.py:34
  177.7 11.5 %fusion.28 = (f32[2]{0:T(128)S(1)}, f32[2,1200]{1,0:T(2,128)}) fusion(f32[1200,2]{0,1:T(2,128)S(1)} %get-tuple-element.10, bf16[9600,2]{0,1:T(2,128)(2,1)S(1)} %reshape.12, bf16[1200,9600]{1,0:T(8,128)(2,1)} %param.7), kind=kOutput, calls=%fused_computation.43 | convolution fusion | flops 46084800 | bytes 23097608 | tf_op jit(solution)/shard_map/wq,aq->wa/dot_general | solution.py:35
  189.6 6.3 %fusion.26 = f32[1200,2,1200]{2,0,1:T(8,128)} fusion(bf16[1200,2,400]{0,2,1:T(8,128)(2,1)S(1)} %get-tuple-element.11, bf16[1200,400]{0,1:T(8,128)(2,1)S(1)} %copy-done), kind=kOutput, calls=%fused_computation.39 | convolution fusion | flops 2304000000 | bytes 14400000 | tf_op jit(solution)/shard_map/awi,bi->wab/dot_general | solution.py:25
  195.9 13.4 %copy.22 = f32[1200,2,1200]{0,2,1:T(8,128)} copy(f32[1200,2,1200]{2,0,1:T(8,128)} %fusion.26) | data formatting | bytes 23040000 | tf_op jit(solution)/shard_map/awi,bi->wab/dot_general | solution.py:25
  209.3 10.9 %fusion.8 = f32[2]{0:T(128)S(1)} fusion(f32[1200,2,1200]{2,0,1:T(8,128)} %fusion.26, f32[1200,2,1200]{0,2,1:T(8,128)} %copy.22, f32[1200,1200]{0,1:T(8,128)} %copy.21), kind=kLoop, calls=%fused_computation.17 | loop fusion | flops 8639998 | bytes 28800008 | tf_op jit(solution)/shard_map/reduce_sum | solution.py:32
  220.3 1.5 collective-permute-start.5
  221.8 8.0 %convolution_bitcast_fusion.3 = f32[2,1200,1200]{2,1,0:T(8,128)} fusion(bf16[1200,2,400]{0,2,1:T(8,128)(2,1)} %collective-permute-done.1, bf16[1200,400]{0,1:T(8,128)(2,1)S(1)} %copy-done), kind=kOutput, calls=%fused_computation.15 | convolution fusion | flops 2304000000 | bytes 14400000 | tf_op jit(solution)/shard_map/ai,bwi->wab/dot_general | solution.py:26
  229.8 8.6 %fusion.17 = f32[2]{0:T(128)S(1)} fusion(f32[2,1200,1200]{2,1,0:T(8,128)} %convolution_bitcast_fusion.3, bf16[1200,2,400]{0,2,1:T(8,128)(2,1)S(1)} %get-tuple-element.11, f32[1200,1200]{1,0:T(8,128)S(1)} %bitcast.102, bf16[1200,400]{0,1:T(8,128)(2,1)S(1)} %copy-done.4), kind=kOutput, calls=%fused_computation.30 | convolution fusion | flops 2312640000 | bytes 20160008 | tf_op jit(solution)/shard_map/awi,bi->wab/dot_general | solution.py:25
  238.4 8.2 %convolution_bitcast_fusion.2 = f32[2,1200,1200]{2,1,0:T(8,128)} fusion(bf16[1200,2,400]{0,2,1:T(8,128)(2,1)} %collective-permute-done.3, bf16[1200,400]{0,1:T(8,128)(2,1)S(1)} %copy-done), kind=kOutput, calls=%fused_computation.14 | convolution fusion | flops 2304000000 | bytes 14400000 | tf_op jit(solution)/shard_map/ai,bwi->wab/dot_general | solution.py:26
  246.9 8.6 %fusion.16 = f32[2]{0:T(128)S(1)} fusion(f32[2,1200,1200]{2,1,0:T(8,128)} %convolution_bitcast_fusion.2, bf16[1200,2,400]{0,2,1:T(8,128)(2,1)S(1)} %get-tuple-element.11, f32[1200,1200]{1,0:T(8,128)S(1)} %bitcast.100, bf16[1200,400]{0,1:T(8,128)(2,1)S(1)} %copy-done.2), kind=kOutput, calls=%fused_computation.29 | convolution fusion | flops 2312640000 | bytes 20160008 | tf_op jit(solution)/shard_map/awi,bi->wab/dot_general | solution.py:25
  255.5 8.1 %convolution_bitcast_fusion.1 = f32[2,1200,1200]{2,1,0:T(8,128)} fusion(bf16[1200,2,400]{0,2,1:T(8,128)(2,1)} %collective-permute-done.5, bf16[1200,400]{0,1:T(8,128)(2,1)S(1)} %copy-done), kind=kOutput, calls=%fused_computation.13 | convolution fusion | flops 2304000000 | bytes 14400000 | tf_op jit(solution)/shard_map/ai,bwi->wab/dot_general | solution.py:26
  263.6 8.9 %fusion.15 = f32[2]{0:T(128)S(1)} fusion(f32[2,1200,1200]{2,1,0:T(8,128)} %convolution_bitcast_fusion.1, bf16[1200,2,400]{0,2,1:T(8,128)(2,1)S(1)} %get-tuple-element.11, f32[1200,1200]{1,0:T(8,128)S(1)} %bitcast.98, bf16[1200,400]{0,1:T(8,128)(2,1)} %collective-permute-done.4), kind=kOutput, calls=%fused_computation.28 | convolution fusion | flops 2312640000 | bytes 20160008 | tf_op jit(solution)/shard_map/awi,bi->wab/dot_general | solution.py:25
  272.7 8.1 %convolution_bitcast_fusion = f32[2,1200,1200]{2,1,0:T(8,128)} fusion(bf16[1200,2,400]{0,2,1:T(8,128)(2,1)} %collective-permute-done.7, bf16[1200,400]{0,1:T(8,128)(2,1)S(1)} %copy-done), kind=kOutput, calls=%fused_computation.12 | convolution fusion | flops 2304000000 | bytes 14400000 | tf_op jit(solution)/shard_map/ai,bwi->wab/dot_general | solution.py:26
  280.8 8.7 %fusion.14 = f32[2]{0:T(128)S(1)} fusion(f32[2,1200,1200]{2,1,0:T(8,128)} %convolution_bitcast_fusion, bf16[1200,2,400]{0,2,1:T(8,128)(2,1)S(1)} %get-tuple-element.11, f32[1200,1200]{1,0:T(8,128)S(1)} %bitcast.96, bf16[1200,400]{0,1:T(8,128)(2,1)} %collective-permute-done.6), kind=kOutput, calls=%fused_computation.27 | convolution fusion | flops 2312640000 | bytes 20160008 | tf_op jit(solution)/shard_map/awi,bi->wab/dot_general | solution.py:25
  289.6 14.5 %all-reduce = (f32[2]{0:T(128)}, f32[2]{0:T(128)}) all-reduce(f32[2]{0:T(128)S(1)} %broadcast_multiply_fusion, f32[2]{0:T(128)S(1)} %add_multiply_fusion), channel_id=1, replica_groups=mesh['pts'=8,'wlk'=4] {'pts'}, use_global_device_ids=true, to_apply=%region_1.2 | all-reduce | flops 4 | bytes 32 | tf_op jit(solution)/shard_map/psum | solution.py:46
  (48 shorter events, 1.8 us)
Async XLA Ops:
  7.2 118.0 %all-gather.3.cloned.1.call-start = ((), (), s32[]{:S(2)}) async-start(), calls=%async_computation | async-start | bytes 7680000 | tf_op jit(solution)/shard_map/all_gather | solution.py:17
  7.9 15.8 %collective-permute-start = (bf16[1200,400]{0,1:T(8,128)(2,1)}, bf16[1200,400]{0,1:T(8,128)(2,1)S(1)}, u32[]{:S(2)}, u32[]{:S(2)}) collective-permute-start(bf16[1200,400]{0,1:T(8,128)(2,1)} %param.6), channel_id=1, source_target_pairs={{28,0},{0,4},{4,8},{8,12},{12,16},{16,20},{20,24},{24,28},{29,1},{... | collective-permute-start | bytes 2880008 | tf_op jit(solution)/shard_map/ppermute | solution.py:10
  23.7 14.9 %copy-start.3 = (bf16[1200,400]{0,1:T(8,128)(2,1)}, bf16[1200,400]{0,1:T(8,128)(2,1)S(1)}, u32[]{:S(2)}) copy-start(bf16[1200,400]{0,1:T(8,128)(2,1)S(1)} %collective-permute-done) | copy-start | bytes 2880004
  23.7 14.9 %collective-permute-start.2 = (bf16[1200,400]{0,1:T(8,128)(2,1)S(1)}, bf16[1200,400]{0,1:T(8,128)(2,1)S(1)}, u32[]{:S(2)}, u32[]{:S(2)}) collective-permute-start(bf16[1200,400]{0,1:T(8,128)(2,1)S(1)} %collective-permute-done), channel_id=1, source_target_pairs={{28,0},{0,4},{4,8},{8,12},{12,16},{16,20},{20,24},{24,28},{29,1},{... | collective-permute-start | bytes 2880008 | tf_op jit(solution)/shard_map/ppermute | solution.py:10
  38.6 96.0 %copy-start.1 = (bf16[1200,400]{0,1:T(8,128)(2,1)}, bf16[1200,400]{0,1:T(8,128)(2,1)S(1)}, u32[]{:S(2)}) copy-start(bf16[1200,400]{0,1:T(8,128)(2,1)S(1)} %collective-permute-done.2) | copy-start | bytes 2880004
  38.6 121.4 %collective-permute-start.4 = (bf16[1200,400]{0,1:T(8,128)(2,1)S(1)}, bf16[1200,400]{0,1:T(8,128)(2,1)}, u32[]{:S(2)}, u32[]{:S(2)}) collective-permute-start(bf16[1200,400]{0,1:T(8,128)(2,1)S(1)} %collective-permute-done.2), channel_id=1, source_target_pairs={{28,0},{0,4},{4,8},{8,12},{12,16},{16,20},{20,24},{24,28},{29,1},{... | collective-permute-start | bytes 2880008 | tf_op jit(solution)/shard_map/ppermute | solution.py:10
  134.6 54.6 %collective-permute-start.1 = (bf16[1200,2,400]{0,2,1:T(8,128)(2,1)S(1)}, bf16[1200,2,400]{0,2,1:T(8,128)(2,1)}, u32[]{:S(2)}, u32[]{:S(2)}) collective-permute-start(bf16[1200,2,400]{0,2,1:T(8,128)(2,1)S(1)} %get-tuple-element.11), channel_id=1, source_target_pairs={{28,0},{0,4},{4,8},{8,12},{12,16},{16,20},{20,24},{24,28},{29,1},{... | collective-permute-start | bytes 5760008 | tf_op jit(solution)/shard_map/ppermute | solution.py:10
  160.0 120.9 %collective-permute-start.6 = (bf16[1200,400]{0,1:T(8,128)(2,1)}, bf16[1200,400]{0,1:T(8,128)(2,1)}, u32[]{:S(2)}, u32[]{:S(2)}) collective-permute-start(bf16[1200,400]{0,1:T(8,128)(2,1)} %collective-permute-done.4), channel_id=1, source_target_pairs={{28,0},{0,4},{4,8},{8,12},{12,16},{16,20},{20,24},{24,28},{29,1},{... | collective-permute-start | bytes 2880008 | tf_op jit(solution)/shard_map/ppermute | solution.py:10
  177.7 11.9 %copy-start = (bf16[1200,400]{0,1:T(8,128)(2,1)S(1)}, bf16[1200,400]{0,1:T(8,128)(2,1)}, u32[]{:S(2)}) copy-start(bf16[1200,400]{0,1:T(8,128)(2,1)} %param.6) | copy-start | bytes 2880004
  189.2 31.0 %collective-permute-start.3 = (bf16[1200,2,400]{0,2,1:T(8,128)(2,1)}, bf16[1200,2,400]{0,2,1:T(8,128)(2,1)}, u32[]{:S(2)}, u32[]{:S(2)}) collective-permute-start(bf16[1200,2,400]{0,2,1:T(8,128)(2,1)} %collective-permute-done.1), channel_id=1, source_target_pairs={{28,0},{0,4},{4,8},{8,12},{12,16},{16,20},{20,24},{24,28},{29,1},{... | collective-permute-start | bytes 5760008 | tf_op jit(solution)/shard_map/ppermute | solution.py:10
  209.3 20.4 %slice-start.6 = ((s8[6144000]{0:T(1024)(128)(4,1)}), s8[4194304]{0:T(1024)(128)(4,1)S(1)}, s32[]{:S(2)}) async-start(s8[6144000]{0:T(1024)(128)(4,1)} %bitcast.101), calls=%async_computation.7 | async-start | bytes 8388608
  220.3 9.5 %slice-start.7 = ((s8[6144000]{0:T(1024)(128)(4,1)}), s8[1949696]{0:T(1024)(128)(4,1)S(1)}, s32[]{:S(2)}) async-start(s8[6144000]{0:T(1024)(128)(4,1)} %bitcast.101), calls=%async_computation.8 | async-start | bytes 3899392
  220.3 9.5 %copy-start.4 = (bf16[1200,400]{0,1:T(8,128)(2,1)S(1)}, bf16[1200,400]{0,1:T(8,128)(2,1)}, u32[]{:S(2)}) copy-start(bf16[1200,400]{0,1:T(8,128)(2,1)} %copy-done.3) | copy-start | bytes 2880004
  220.3 26.3 %collective-permute-start.5 = (bf16[1200,2,400]{0,2,1:T(8,128)(2,1)}, bf16[1200,2,400]{0,2,1:T(8,128)(2,1)}, u32[]{:S(2)}, u32[]{:S(2)}) collective-permute-start(bf16[1200,2,400]{0,2,1:T(8,128)(2,1)} %collective-permute-done.3), channel_id=1, source_target_pairs={{28,0},{0,4},{4,8},{8,12},{12,16},{16,20},{20,24},{24,28},{29,1},{... | collective-permute-start | bytes 5760008 | tf_op jit(solution)/shard_map/ppermute | solution.py:10
  229.8 17.1 %slice-start.4 = ((s8[6144000]{0:T(1024)(128)(4,1)}), s8[4194304]{0:T(1024)(128)(4,1)S(1)}, s32[]{:S(2)}) async-start(s8[6144000]{0:T(1024)(128)(4,1)} %bitcast.99), calls=%async_computation.5 | async-start | bytes 8388608
  238.4 8.5 %slice-start.5 = ((s8[6144000]{0:T(1024)(128)(4,1)}), s8[1949696]{0:T(1024)(128)(4,1)S(1)}, s32[]{:S(2)}) async-start(s8[6144000]{0:T(1024)(128)(4,1)} %bitcast.99), calls=%async_computation.6 | async-start | bytes 3899392
  238.4 8.5 %copy-start.2 = (bf16[1200,400]{0,1:T(8,128)(2,1)S(1)}, bf16[1200,400]{0,1:T(8,128)(2,1)}, u32[]{:S(2)}) copy-start(bf16[1200,400]{0,1:T(8,128)(2,1)} %copy-done.1) | copy-start | bytes 2880004
  246.6 26.1 %collective-permute-start.7 = (bf16[1200,2,400]{0,2,1:T(8,128)(2,1)}, bf16[1200,2,400]{0,2,1:T(8,128)(2,1)}, u32[]{:S(2)}, u32[]{:S(2)}) collective-permute-start(bf16[1200,2,400]{0,2,1:T(8,128)(2,1)} %collective-permute-done.5), channel_id=1, source_target_pairs={{28,0},{0,4},{4,8},{8,12},{12,16},{16,20},{20,24},{24,28},{29,1},{... | collective-permute-start | bytes 5760008 | tf_op jit(solution)/shard_map/ppermute | solution.py:10
  246.9 16.7 %slice-start.2 = ((s8[6144000]{0:T(1024)(128)(4,1)}), s8[4194304]{0:T(1024)(128)(4,1)S(1)}, s32[]{:S(2)}) async-start(s8[6144000]{0:T(1024)(128)(4,1)} %bitcast.97), calls=%async_computation.3 | async-start | bytes 8388608
  255.5 8.2 %slice-start.3 = ((s8[6144000]{0:T(1024)(128)(4,1)}), s8[1949696]{0:T(1024)(128)(4,1)S(1)}, s32[]{:S(2)}) async-start(s8[6144000]{0:T(1024)(128)(4,1)} %bitcast.97), calls=%async_computation.4 | async-start | bytes 3899392
  263.6 17.2 %slice-start = ((s8[6144000]{0:T(1024)(128)(4,1)}), s8[4194304]{0:T(1024)(128)(4,1)S(1)}, s32[]{:S(2)}) async-start(s8[6144000]{0:T(1024)(128)(4,1)} %bitcast.95), calls=%async_computation.1 | async-start | bytes 8388608
  272.5 8.3 %slice-start.1 = ((s8[6144000]{0:T(1024)(128)(4,1)}), s8[1949696]{0:T(1024)(128)(4,1)S(1)}, s32[]{:S(2)}) async-start(s8[6144000]{0:T(1024)(128)(4,1)} %bitcast.95), calls=%async_computation.2 | async-start | bytes 3899392
Sparse Core Ops, SparseCore 0:
  9.5 115.6 all-gather.2
where the time goes:
time: 312 us; the launch traced here: 311 us
  waiting for transfers between devices  115 us (37%)
  matrix products  94.4 us (30%)
  other arithmetic  31.5 us (10%)
  blocking collectives  30.5 us (10%)
  local copies, waits for them, and re-layouts  21.5 us (7%)
  between operations  14.1 us (5%)
  starting transfers between devices  4.4 us (1%)
    all_gather x1, waiting for transfers between devices, local(): lax.all_gather(collocation, 'wlk', axis=0, tiled=True)  86.6 us
    dot_general x5, matrix products, block_terms(): jnp.einsum('awi,bi->wab', theta, occ_far, preferred_element_type=jnp.floa...  41.1 us
    dot_general x4, matrix products, block_terms(): jnp.einsum('ai,bwi->wab', occupied, theta_far, preferred_element_type=jnp...  32.4 us
    ppermute x8, waiting for transfers between devices, passed_along(): return lax.ppermute(block, axis, route)  27.3 us
    convert_element_type x1, other arithmetic, block_terms(): lax.dynamic_slice_in_dim(kernel, start, occ_far.shape[0], 1)  17.5 us
    all_gather x1, blocking collectives, local(): density_all = lax.all_gather(density_b, 'pts', axis=1, tiled=True)  16 us
    psum x1, blocking collectives, local(): lax.psum((coulomb, -0.5 * exchange_sum), 'pts')  14.5 us
    dot_general x1, local copies, waits for them, and re-layouts, block_terms(): jnp.einsum('awi,bi->wab', theta, occ_far, preferred_element_type=jnp.floa...  13.4 us
  transfers between devices with their start and end apart: 9, of which 4 were waited for; matrix products, arithmetic and copies ran while one was open for 45% of the time, Pallas kernels for 0%

commit v1 on v0

v1 whole, which is shorter than its diff:
```python
import functools

import jax
import jax.numpy as jnp
from jax import lax
from jax.experimental import pallas as pl
from jax.experimental.pallas import tpu as pltpu
from jax.sharding import PartitionSpec as P

NT = (((1,), (1,)), ((), ()))


def tile_of(points):
    return max(t for t in range(8, 257, 8) if points % t == 0)


def exchange_kernel(walkers, first_ref, near_ref, occ_near_ref, far_ref, occ_far_ref, k_ref, out_ref):
    @pl.when(pl.program_id(0) == 0)
    def _():
        out_ref[...] = jnp.zeros_like(out_ref)

    rows = occ_near_ref.shape[0]
    width = k_ref.shape[2]
    kern = k_ref[0].astype(jnp.float32)
    for w in range(walkers):
        near = lax.dot_general(near_ref[w], occ_far_ref[...], NT, preferred_element_type=jnp.float32)
        far = lax.dot_general(occ_near_ref[...], far_ref[w], NT, preferred_element_type=jnp.float32)
        out_ref[w] += jnp.sum((kern * near * far).reshape(rows // 8, 8, width), axis=0)


def exchange_block(first_tile, theta, occupied, theta_far, occ_far, tiles):
    walkers, rows, elec = theta.shape
    width = tiles.shape[2]
    steps = occ_far.shape[0] // width
    out = pl.pallas_call(
        functools.partial(exchange_kernel, walkers),
        out_shape=jax.ShapeDtypeStruct((walkers, 8, width), jnp.float32),
        grid_spec=pltpu.PrefetchScalarGridSpec(
            num_scalar_prefetch=1,
            grid=(steps,),
            in_specs=[
                pl.BlockSpec((walkers, rows, elec), lambda j, s: (0, 0, 0)),
                pl.BlockSpec((rows, elec), lambda j, s: (0, 0)),
                pl.BlockSpec((walkers, width, elec), lambda j, s: (0, j, 0)),
                pl.BlockSpec((width, elec), lambda j, s: (j, 0)),
                pl.BlockSpec((1, rows, width), lambda j, s: (s[0] + j, 0, 0)),
            ],
            out_specs=pl.BlockSpec((walkers, 8, width), lambda j, s: (0, 0, 0)),
        ),
        compiler_params=pltpu.CompilerParams(vmem_limit_bytes=48 * 1024 * 1024),
        cost_estimate=pl.CostEstimate(
            flops=2 * walkers * 2 * rows * occ_far.shape[0] * elec * 2,
            bytes_accessed=2 * rows * occ_far.shape[0],
            transcendentals=0,
        ),
        name="exchange",
    )(first_tile.reshape(1).astype(jnp.int32), theta, occupied, theta_far, occ_far, tiles)
    return jnp.sum(out, axis=(1, 2))


def shifted(block, distance):
    devices = lax.axis_size("pts")
    return lax.ppermute(block, "pts", [((i - distance) % devices, i) for i in range(devices)])


def local(green_half, collocation, occupied, kernel):
    rows, elec = occupied.shape
    devices = lax.axis_size("pts")
    position = lax.axis_index("pts")
    width = tile_of(rows)
    per_block = rows // width
    first = (per_block + 1) // 2
    spans = ((0, first), (first, per_block))
    tiles = kernel.reshape(rows, kernel.shape[1] // width, width).transpose(1, 0, 2)
    far_counts = range(1, devices // 2 + 1)

    occ_far = {}
    travel = occupied
    for stride in far_counts:
        travel = shifted(travel, 1)
        occ_far[stride] = travel

    parts = []
    for low, high in spans:
        points = collocation[:, low * width : high * width]
        gathered = lax.all_gather(points, "wlk", axis=0, tiled=True)
        parts.append(
            jnp.einsum("mp,wim->wpi", gathered, green_half, preferred_element_type=jnp.float32).astype(
                jnp.bfloat16
            )
        )
    theta = jnp.concatenate(parts, axis=1)

    far_parts = [{}, {}]
    for h in range(2):
        travel = parts[h]
        for stride in far_counts:
            travel = shifted(travel, 1)
            far_parts[h][stride] = travel

    density = jnp.einsum("wpi,pi->wp", theta, occupied, preferred_element_type=jnp.float32)
    density_b = density.astype(jnp.bfloat16)
    density_all = lax.all_gather(density_b, "pts", axis=1, tiled=True)
    potential = jnp.einsum("wq,aq->wa", density_all, kernel, preferred_element_type=jnp.float32)

    exchange_sum = exchange_block(position * per_block, theta, occupied, theta, occupied, tiles)
    for h, (low, high) in enumerate(spans):
        for stride in far_counts:
            source = (position - stride) % devices
            weight = 1.0 if 2 * stride == devices else 2.0
            exchange_sum = exchange_sum + weight * exchange_block(
                source * per_block + low,
                theta,
                occupied,
                far_parts[h][stride],
                occ_far[stride][low * width : high * width],
                tiles,
            )
    coulomb = 0.5 * jnp.sum(density * potential, axis=1)
    coulomb_energy, exchange_energy = lax.psum((coulomb, -0.5 * exchange_sum), "pts")
    return (potential, coulomb_energy, exchange_energy)


def solution(mesh):
    placed = (P("wlk", None, None), P("wlk", "pts"), P("pts", None), P("pts", None))
    return jax.shard_map(
        local,
        mesh=mesh,
        in_specs=placed,
        out_specs=(P("wlk", "pts"), P("wlk"), P("wlk")),
        check_vma=False,
    )
```

time: 312 us -> 329 us (1.054)
  local copies, waits for them, and re-layouts: 21.5 us -> 133 us
  matrix products: 94.4 us -> 24.2 us
  Pallas kernels: 0 us -> 47.8 us
  waiting for transfers between devices: 115 us -> 68.8 us
  other arithmetic: 31.5 us -> 3.74 us
    reshape x0 -> x2, local copies, waits for them, and re-layouts: none -> 72 us  [local(): kernel.reshape(rows, kernel.shape[1] // width, width).transpose(1, 0, 2)]
    dot_general x10 -> x2, matrix products: 82.9 us -> 12.7 us  [local(): jnp.einsum('mp,wim->wpi', gathered, green_half, preferred_element_type=jn...]
    all_gather x1 -> x2, waiting for transfers between devices: 86.6 us -> 23.1 us  [local(): gathered = lax.all_gather(points, 'wlk', axis=0, tiled=True)]
    pallas_call x0 -> x9, Pallas kernels: none -> 47.8 us  [exchange_block(): pl.pallas_call(functools.partial(exchange_kernel, walkers), out_shape=jax...]
    unnamed x27 -> x67, local copies, waits for them, and re-layouts: 0.21 us -> 31.4 us
    ppermute x8 -> x12, waiting for transfers between devices: 27.3 us -> 45.7 us  [shifted(): lax.ppermute(block, 'pts', [((i - distance) % devices, i) for i in range(...]
    convert_element_type x1 -> x0, other arithmetic: 17.5 us -> none  [block_terms(): lax.dynamic_slice_in_dim(kernel, start, occ_far.shape[0], 1)]
    ppermute x0 -> x8, local copies, waits for them, and re-layouts: none -> 17 us  [shifted(): lax.ppermute(block, 'pts', [((i - distance) % devices, i) for i in range(...]
  transfers between devices with their start and end apart: 9 -> 14, of which waited for: 4 -> 6; matrix products, arithmetic and copies ran while one was open for 45% -> 42% of each run, Pallas kernels for 0% -> 13%
where the time goes in v1:
time: 329 us; the launch traced here: 326 us
  local copies, waits for them, and re-layouts  133 us (40%)
  waiting for transfers between devices  68.8 us (21%)
  Pallas kernels  47.8 us (15%)
  blocking collectives  31.8 us (10%)
  matrix products  24.2 us (7%)
  between operations  14.4 us (4%)
  other arithmetic  3.74 us (1%)
    reshape x2, local copies, waits for them, and re-layouts, local(): kernel.reshape(rows, kernel.shape[1] // width, width).transpose(1, 0, 2)  72 us
    pallas_call x9, Pallas kernels, exchange_block(): pl.pallas_call(functools.partial(exchange_kernel, walkers), out_shape=jax...  47.8 us
    ppermute x12, waiting for transfers between devices, shifted(): lax.ppermute(block, 'pts', [((i - distance) % devices, i) for i in range(...  45.7 us
    unnamed x67, local copies, waits for them, and re-layouts  31.4 us
    all_gather x2, waiting for transfers between devices, local(): gathered = lax.all_gather(points, 'wlk', axis=0, tiled=True)  23.1 us
    ppermute x8, local copies, waits for them, and re-layouts, shifted(): lax.ppermute(block, 'pts', [((i - distance) % devices, i) for i in range(...  17 us
    all_gather x1, blocking collectives, local(): density_all = lax.all_gather(density_b, 'pts', axis=1, tiled=True)  16.9 us
    psum x1, blocking collectives, local(): lax.psum((coulomb, -0.5 * exchange_sum), 'pts')  14.9 us
  transfers between devices with their start and end apart: 14, of which 6 were waited for; matrix products, arithmetic and copies ran while one was open for 42% of the time, Pallas kernels for 13%

profile of v1, /device:TPU:0, one launch (start us, length us, event | category | flops | bytes accessed | tf_op | source)
XLA Modules:
  0.0 326.3 jit_solution(14809781916255678776)
XLA Ops:
  11.2 15.1 %collective-permute-done.1 = bf16[1200,400]{0,1:T(8,128)(2,1)S(1)} collective-permute-done((bf16[1200,400]{0,1:T(8,128)(2,1)S(1)}, bf16[1200,400]{0,1:T(8,128)(2,1)S(1)}, u32[]{:S(2)}, u32[]{:S(2)}) %collective-permute-start.1) | collective-permute-done | bytes 960032 | tf_op jit(solution)/shard_map/ppermute | solution.py:63
  26.3 15.0 %collective-permute-done.3 = bf16[1200,400]{0,1:T(8,128)(2,1)} collective-permute-done((bf16[1200,400]{0,1:T(8,128)(2,1)S(1)}, bf16[1200,400]{0,1:T(8,128)(2,1)}, u32[]{:S(2)}, u32[]{:S(2)}) %collective-permute-start.3) | collective-permute-done | bytes 960032 | tf_op jit(solution)/shard_map/ppermute | solution.py:63
  41.3 23.1 %all-gather.6.cloned.1.call-done = bf16[2400,480]{1,0:T(8,128)(2,1)} async-done(((bf16[600,480]{1,0:T(8,128)(2,1)}), bf16[2400,480]{1,0:T(8,128)(2,1)}) %all-gather.6.cloned.1.call-update) | async-done | bytes 2304016 | tf_op jit(solution)/shard_map/all_gather | solution.py:86
  64.4 5.2 %fusion.7 = bf16[2,400,480]{2,1,0:T(8,128)(2,1)S(1)} fusion(bf16[2,400,2400]{2,1,0:T(8,128)(2,1)} %param.4, bf16[2400,480]{1,0:T(8,128)(2,1)} %all-gather.6.cloned.1.call-done), kind=kOutput, calls=%fused_computation.8 | convolution fusion | flops 1843584000 | bytes 6912000 | tf_op jit(solution)/shard_map/mp,wim->wpi/dot_general | solution.py:88
  71.2 11.2 %collective-permute-done.8 = bf16[2,480,400]{1,2,0:T(8,128)(2,1)} collective-permute-done((bf16[2,480,400]{1,2,0:T(8,128)(2,1)S(1)}, bf16[2,480,400]{1,2,0:T(8,128)(2,1)}, u32[]{:S(2)}, u32[]{:S(2)}) %collective-permute-start.8) | collective-permute-done | bytes 768032 | tf_op jit(solution)/shard_map/ppermute | solution.py:63
  85.7 49.8 %reshape.37 = bf16[1200,40,240]{2,1,0:T(8,128)(2,1)} reshape(bf16[1200,9600]{1,0:T(8,128)(2,1)} %param.7) | data formatting | bytes 46080000 | tf_op jit(solution)/shard_map/reshape | solution.py:74
  135.6 22.2 %copy.116 = bf16[1200,40,240]{2,0,1:T(8,128)(2,1)} copy(bf16[1200,40,240]{2,1,0:T(8,128)(2,1)} %reshape.37) | data formatting | bytes 46080000 | tf_op jit(solution)/shard_map/reshape | solution.py:74
  177.1 7.6 %fusion.4 = bf16[2,400,720]{2,1,0:T(8,128)(2,1)} fusion(bf16[2,400,2400]{2,1,0:T(8,128)(2,1)} %param.4, bf16[2400,720]{1,0:T(8,128)(2,1)} %all-gather.4.cloned.1.call-done), kind=kOutput, calls=%fused_computation.7 | convolution fusion | flops 2765376000 | bytes 8448000 | tf_op jit(solution)/shard_map/mp,wim->wpi/dot_general | solution.py:88
  191.0 16.9 %all-gather = bf16[8,1200,2]{1,2,0:T(2,128)(2,1)S(1)} all-gather(bf16[1,1200,2]{1,2,0:T(2,128)(2,1)S(1)} %fusion.11), channel_id=1, replica_groups=mesh['pts'=8,'wlk'=4] {'pts'}, dimensions={0}, use_global_device_ids=true | all-gather | bytes 43200 | tf_op jit(solution)/shard_map/all_gather | solution.py:103
  208.1 11.5 %fusion.10 = (f32[2]{0:T(128)S(1)}, f32[2,1200]{1,0:T(2,128)}) fusion(f32[1200,2]{0,1:T(2,128)S(1)} %multiply_reduce_fusion, bf16[9600,2]{0,1:T(2,128)(2,1)S(1)} %reshape.47, bf16[1200,9600]{1,0:T(8,128)(2,1)} %param.7), kind=kOutput, calls=%fused_computation.11 | convolution fusion | flops 46084800 | bytes 23097608 | tf_op jit(solution)/shard_map/wq,aq->wa/dot_general | solution.py:104
  219.8 8.9 %exchange.9 = f32[2,8,240]{2,1,0:T(8,128)S(1)} custom-call(s32[1]{0:T(128)} %bitcast.8.first_ref, bf16[2,1200,400]{2,1,0:T(8,128)(2,1)S(1)} %pad_maximum_fusion.near_ref.far_ref, bf16[1200,400]{1,0:T(8,128)(2,1)S(1)} %copy-done, bf16[2,1200,400]{2,1,0:T(8,128)(2,1)S(1)} %pad_maximum_fusion.near_ref.far_ref, bf16[1200,400]{1,0:T(8,128)(2,1)S(1)} %copy-done, ...), custom_call_target="tpu_custom_call" | custom-call | flops 9216000000 | bytes 2880000 | tf_op jit(solution)/shard_map/exchange/pallas_call | solution.py:35
  228.8 4.2 %exchange.15 = f32[2,8,240]{2,1,0:T(8,128)S(1)} custom-call(s32[1]{0:T(128)} %bitcast.17.first_ref, bf16[2,1200,400]{2,1,0:T(8,128)(2,1)S(1)} %pad_maximum_fusion.near_ref.far_ref, bf16[1200,400]{1,0:T(8,128)(2,1)S(1)} %copy-done, bf16[2,480,400]{2,1,0:T(8,128)(2,1)S(1)} %copy-done.12, bf16[480,400]{1,0:T(8,128)(2,1)S(1)} %copy-done.20, ...), custom_call_target="tpu_custom_call" | custom-call | flops 3686400000 | bytes 1152000 | tf_op jit(solution)/shard_map/exchange/pallas_call | solution.py:35
  233.0 4.0 %collective-permute-done.2 = bf16[2,720,400]{1,2,0:T(8,128)(2,1)} collective-permute-done((bf16[2,720,400]{1,2,0:T(8,128)(2,1)}, bf16[2,720,400]{1,2,0:T(8,128)(2,1)}, u32[]{:S(2)}, u32[]{:S(2)}) %collective-permute-start.2) | collective-permute-done | bytes 1152032 | tf_op jit(solution)/shard_map/ppermute | solution.py:63
  239.3 4.1 %exchange.14 = f32[2,8,240]{2,1,0:T(8,128)S(1)} custom-call(s32[1]{0:T(128)} %bitcast.15.first_ref, bf16[2,1200,400]{2,1,0:T(8,128)(2,1)S(1)} %pad_maximum_fusion.near_ref.far_ref, bf16[1200,400]{1,0:T(8,128)(2,1)S(1)} %copy-done.1, bf16[2,480,400]{2,1,0:T(8,128)(2,1)S(1)} %copy.89.far_ref, bf16[480,400]{1,0:T(8,128)(2,1)S(1)} %copy-done.19, ...), custom_call_target="tpu_custom_call" | custom-call | flops 3686400000 | bytes 1152000 | tf_op jit(solution)/shard_map/exchange/pallas_call | solution.py:35
  247.4 4.1 %exchange.16 = f32[2,8,240]{2,1,0:T(8,128)S(1)} custom-call(s32[1]{0:T(128)} %bitcast.18.first_ref, bf16[2,1200,400]{2,1,0:T(8,128)(2,1)S(1)} %pad_maximum_fusion.near_ref.far_ref, bf16[1200,400]{1,0:T(8,128)(2,1)S(1)} %copy-done.2, bf16[2,480,400]{2,1,0:T(8,128)(2,1)S(1)} %copy.95.far_ref, bf16[480,400]{1,0:T(8,128)(2,1)S(1)} %copy-done.18, ...), custom_call_target="tpu_custom_call" | custom-call | flops 3686400000 | bytes 1152000 | tf_op jit(solution)/shard_map/exchange/pallas_call | solution.py:35
  251.6 2.6 copy.76.far_ref
  256.9 5.6 %exchange.10 = f32[2,8,240]{2,1,0:T(8,128)S(1)} custom-call(s32[1]{0:T(128)} %bitcast.10.first_ref, bf16[2,1200,400]{2,1,0:T(8,128)(2,1)S(1)} %pad_maximum_fusion.near_ref.far_ref, bf16[1200,400]{1,0:T(8,128)(2,1)S(1)} %copy-done.3, bf16[2,720,400]{2,1,0:T(8,128)(2,1)S(1)} %copy-done.9, bf16[720,400]{1,0:T(8,128)(2,1)S(1)} %copy-done.16, ...), custom_call_target="tpu_custom_call" | custom-call | flops 5529600000 | bytes 1728000 | tf_op jit(solution)/shard_map/exchange/pallas_call | solution.py:35
  267.2 4.1 %exchange.17 = f32[2,8,240]{2,1,0:T(8,128)S(1)} custom-call(s32[1]{0:T(128)} %bitcast.19.first_ref, bf16[2,1200,400]{2,1,0:T(8,128)(2,1)S(1)} %pad_maximum_fusion.near_ref.far_ref, bf16[1200,400]{1,0:T(8,128)(2,1)S(1)} %copy-done.4, bf16[2,480,400]{2,1,0:T(8,128)(2,1)S(1)} %copy.98.far_ref, bf16[480,400]{1,0:T(8,128)(2,1)S(1)} %copy-done.17, ...), custom_call_target="tpu_custom_call" | custom-call | flops 3686400000 | bytes 1152000 | tf_op jit(solution)/shard_map/exchange/pallas_call | solution.py:35
  271.4 2.6 copy.79.far_ref
  276.7 5.6 %exchange.11 = f32[2,8,240]{2,1,0:T(8,128)S(1)} custom-call(s32[1]{0:T(128)} %bitcast.12.first_ref, bf16[2,1200,400]{2,1,0:T(8,128)(2,1)S(1)} %pad_maximum_fusion.near_ref.far_ref, bf16[1200,400]{1,0:T(8,128)(2,1)S(1)} %copy-done.5, bf16[2,720,400]{2,1,0:T(8,128)(2,1)S(1)} %copy-done.10, bf16[720,400]{1,0:T(8,128)(2,1)S(1)} %copy-done.14, ...), custom_call_target="tpu_custom_call" | custom-call | flops 5529600000 | bytes 1728000 | tf_op jit(solution)/shard_map/exchange/pallas_call | solution.py:35
  282.4 2.6 copy.82.far_ref
  287.7 5.6 %exchange.12 = f32[2,8,240]{2,1,0:T(8,128)S(1)} custom-call(s32[1]{0:T(128)} %bitcast.13.first_ref, bf16[2,1200,400]{2,1,0:T(8,128)(2,1)S(1)} %pad_maximum_fusion.near_ref.far_ref, bf16[1200,400]{1,0:T(8,128)(2,1)S(1)} %copy-done.6, bf16[2,720,400]{2,1,0:T(8,128)(2,1)S(1)} %copy-done.11, bf16[720,400]{1,0:T(8,128)(2,1)S(1)} %copy-done.15, ...), custom_call_target="tpu_custom_call" | custom-call | flops 5529600000 | bytes 1728000 | tf_op jit(solution)/shard_map/exchange/pallas_call | solution.py:35
  298.8 5.6 %exchange.13 = f32[2,8,240]{2,1,0:T(8,128)S(1)} custom-call(s32[1]{0:T(128)} %bitcast.14.first_ref, bf16[2,1200,400]{2,1,0:T(8,128)(2,1)S(1)} %pad_maximum_fusion.near_ref.far_ref, bf16[1200,400]{1,0:T(8,128)(2,1)S(1)} %copy-done.7, bf16[2,720,400]{2,1,0:T(8,128)(2,1)S(1)} %copy-done.8, bf16[720,400]{1,0:T(8,128)(2,1)S(1)} %copy-done.13, ...), custom_call_target="tpu_custom_call" | custom-call | flops 5529600000 | bytes 1728000 | tf_op jit(solution)/shard_map/exchange/pallas_call | solution.py:35
  304.5 14.9 %all-reduce = (f32[2]{0:T(128)}, f32[2]{0:T(128)}) all-reduce(f32[2]{0:T(128)S(1)} %get-tuple-element.8, f32[2]{0:T(128)S(1)} %get-tuple-element.7), channel_id=1, replica_groups=mesh['pts'=8,'wlk'=4] {'pts'}, use_global_device_ids=true, to_apply=%region_1.2 | all-reduce | flops 4 | bytes 32 | tf_op jit(solution)/shard_map/psum | solution.py:120
  (123 shorter events, 59.8 us)
Async XLA Ops:
  7.2 3.5 %copy-start.24 = (bf16[1200,400]{0,1:T(8,128)(2,1)S(1)}, bf16[1200,400]{0,1:T(8,128)(2,1)}, u32[]{:S(2)}) copy-start(bf16[1200,400]{0,1:T(8,128)(2,1)} %param.6) | copy-start | bytes 2880004
  7.2 57.2 %all-gather.6.cloned.1.call-start = ((), (), s32[]{:S(2)}) async-start(), calls=%async_computation.1 | async-start | bytes 3072000 | tf_op jit(solution)/shard_map/all_gather | solution.py:86
  9.6 167.4 %all-gather.4.cloned.1.call-start = ((), (), s32[]{:S(2)}) async-start(), calls=%async_computation | async-start | bytes 4608000 | tf_op jit(solution)/shard_map/all_gather | solution.py:86
  10.7 15.6 %collective-permute-start.1 = (bf16[1200,400]{0,1:T(8,128)(2,1)S(1)}, bf16[1200,400]{0,1:T(8,128)(2,1)S(1)}, u32[]{:S(2)}, u32[]{:S(2)}) collective-permute-start(bf16[1200,400]{0,1:T(8,128)(2,1)S(1)} %copy-done.24), channel_id=1, source_target_pairs={{28,0},{0,4},{4,8},{8,12},{12,16},{16,20},{20,24},{24,28},{29,1},{... | collective-permute-start | bytes 2880008 | tf_op jit(solution)/shard_map/ppermute | solution.py:63
  26.3 15.0 %collective-permute-start.3 = (bf16[1200,400]{0,1:T(8,128)(2,1)S(1)}, bf16[1200,400]{0,1:T(8,128)(2,1)}, u32[]{:S(2)}, u32[]{:S(2)}) collective-permute-start(bf16[1200,400]{0,1:T(8,128)(2,1)S(1)} %collective-permute-done.1), channel_id=1, source_target_pairs={{28,0},{0,4},{4,8},{8,12},{12,16},{16,20},{20,24},{24,28},{29,1},{... | collective-permute-start | bytes 2880008 | tf_op jit(solution)/shard_map/ppermute | solution.py:63
  41.3 28.3 %collective-permute-start.5 = (bf16[1200,400]{0,1:T(8,128)(2,1)}, bf16[1200,400]{0,1:T(8,128)(2,1)S(1)}, u32[]{:S(2)}, u32[]{:S(2)}) collective-permute-start(bf16[1200,400]{0,1:T(8,128)(2,1)} %collective-permute-done.3), channel_id=1, source_target_pairs={{28,0},{0,4},{4,8},{8,12},{12,16},{16,20},{20,24},{24,28},{29,1},{... | collective-permute-start | bytes 2880008 | tf_op jit(solution)/shard_map/ppermute | solution.py:63
  69.5 12.8 %collective-permute-start.8 = (bf16[2,480,400]{1,2,0:T(8,128)(2,1)S(1)}, bf16[2,480,400]{1,2,0:T(8,128)(2,1)}, u32[]{:S(2)}, u32[]{:S(2)}) collective-permute-start(bf16[2,480,400]{1,2,0:T(8,128)(2,1)S(1)} %bitcast.58), channel_id=1, source_target_pairs={{28,0},{0,4},{4,8},{8,12},{12,16},{16,20},{20,24},{24,28},{29,1},{... | collective-permute-start | bytes 2304008 | tf_op jit(solution)/shard_map/ppermute | solution.py:63
  70.4 97.8 %collective-permute-start.7 = (bf16[1200,400]{0,1:T(8,128)(2,1)S(1)}, bf16[1200,400]{0,1:T(8,128)(2,1)}, u32[]{:S(2)}, u32[]{:S(2)}) collective-permute-start(bf16[1200,400]{0,1:T(8,128)(2,1)S(1)} %collective-permute-done.5), channel_id=1, source_target_pairs={{28,0},{0,4},{4,8},{8,12},{12,16},{16,20},{20,24},{24,28},{29,1},{... | collective-permute-start | bytes 2880008 | tf_op jit(solution)/shard_map/ppermute | solution.py:63
  82.4 91.8 %collective-permute-start.9 = (bf16[2,480,400]{1,2,0:T(8,128)(2,1)}, bf16[2,480,400]{1,2,0:T(8,128)(2,1)}, u32[]{:S(2)}, u32[]{:S(2)}) collective-permute-start(bf16[2,480,400]{1,2,0:T(8,128)(2,1)} %collective-permute-done.8), channel_id=1, source_target_pairs={{28,0},{0,4},{4,8},{8,12},{12,16},{16,20},{20,24},{24,28},{29,1},{... | collective-permute-start | bytes 2304008 | tf_op jit(solution)/shard_map/ppermute | solution.py:63
  163.6 3.4 %copy-start.27 = (bf16[2,400,480]{2,1,0:T(8,128)(2,1)S(1)}, bf16[2,400,480]{2,1,0:T(8,128)(2,1)}, u32[]{:S(2)}) copy-start(bf16[2,400,480]{2,1,0:T(8,128)(2,1)} %copy-done.26) | copy-start | bytes 2304004
  174.1 69.5 %collective-permute-start.10 = (bf16[2,480,400]{1,2,0:T(8,128)(2,1)}, bf16[2,480,400]{1,2,0:T(8,128)(2,1)}, u32[]{:S(2)}, u32[]{:S(2)}) collective-permute-start(bf16[2,480,400]{1,2,0:T(8,128)(2,1)} %collective-permute-done.9), channel_id=1, source_target_pairs={{28,0},{0,4},{4,8},{8,12},{12,16},{16,20},{20,24},{24,28},{29,1},{... | collective-permute-start | bytes 2304008 | tf_op jit(solution)/shard_map/ppermute | solution.py:63
  187.2 32.4 %collective-permute-start = (bf16[2,720,400]{1,2,0:T(8,128)(2,1)}, bf16[2,720,400]{1,2,0:T(8,128)(2,1)}, u32[]{:S(2)}, u32[]{:S(2)}) collective-permute-start(bf16[2,720,400]{1,2,0:T(8,128)(2,1)} %bitcast.11), channel_id=1, source_target_pairs={{28,0},{0,4},{4,8},{8,12},{12,16},{16,20},{20,24},{24,28},{29,1},{... | collective-permute-start | bytes 3456008 | tf_op jit(solution)/shard_map/ppermute | solution.py:63
  187.3 2.9 copy-start.22
  187.3 3.1 copy-start.23
  208.1 11.7 %copy-start = (bf16[1200,400]{1,0:T(8,128)(2,1)S(1)}, bf16[1200,400]{1,0:T(8,128)(2,1)}, u32[]{:S(2)}) copy-start(bf16[1200,400]{1,0:T(8,128)(2,1)} %copy.71.occ_near_ref.occ_far_ref) | copy-start | bytes 2880004
  219.6 17.4 %collective-permute-start.2 = (bf16[2,720,400]{1,2,0:T(8,128)(2,1)}, bf16[2,720,400]{1,2,0:T(8,128)(2,1)}, u32[]{:S(2)}, u32[]{:S(2)}) collective-permute-start(bf16[2,720,400]{1,2,0:T(8,128)(2,1)} %collective-permute-done), channel_id=1, source_target_pairs={{28,0},{0,4},{4,8},{8,12},{12,16},{16,20},{20,24},{24,28},{29,1},{... | collective-permute-start | bytes 3456008 | tf_op jit(solution)/shard_map/ppermute | solution.py:63
  219.8 8.9 %copy-start.12 = (bf16[2,480,400]{2,1,0:T(8,128)(2,1)S(1)}, bf16[2,480,400]{2,1,0:T(8,128)(2,1)}, u32[]{:S(2)}) copy-start(bf16[2,480,400]{2,1,0:T(8,128)(2,1)} %copy.92.far_ref) | copy-start | bytes 2304004
  219.8 9.0 %copy-start.20 = (bf16[480,400]{1,0:T(8,128)(2,1)S(1)}, bf16[480,400]{1,0:T(8,128)(2,1)}, u32[]{:S(2)}) copy-start(bf16[480,400]{1,0:T(8,128)(2,1)} %copy.111.occ_far_ref) | copy-start | bytes 1152004
  237.0 27.6 %collective-permute-start.4 = (bf16[2,720,400]{1,2,0:T(8,128)(2,1)}, bf16[2,720,400]{1,2,0:T(8,128)(2,1)}, u32[]{:S(2)}, u32[]{:S(2)}) collective-permute-start(bf16[2,720,400]{1,2,0:T(8,128)(2,1)} %collective-permute-done.2), channel_id=1, source_target_pairs={{28,0},{0,4},{4,8},{8,12},{12,16},{16,20},{20,24},{24,28},{29,1},{... | collective-permute-start | bytes 3456008 | tf_op jit(solution)/shard_map/ppermute | solution.py:63
  243.6 19.5 %collective-permute-start.11 = (bf16[2,480,400]{1,2,0:T(8,128)(2,1)}, bf16[2,480,400]{1,2,0:T(8,128)(2,1)}, u32[]{:S(2)}, u32[]{:S(2)}) collective-permute-start(bf16[2,480,400]{1,2,0:T(8,128)(2,1)} %collective-permute-done.10), channel_id=1, source_target_pairs={{28,0},{0,4},{4,8},{8,12},{12,16},{16,20},{20,24},{24,28},{29,1},{... | collective-permute-start | bytes 2304008 | tf_op jit(solution)/shard_map/ppermute | solution.py:63
  251.5 2.7 copy-start.16
  264.6 28.9 %collective-permute-start.6 = (bf16[2,720,400]{1,2,0:T(8,128)(2,1)}, bf16[2,720,400]{1,2,0:T(8,128)(2,1)}, u32[]{:S(2)}, u32[]{:S(2)}) collective-permute-start(bf16[2,720,400]{1,2,0:T(8,128)(2,1)} %collective-permute-done.4), channel_id=1, source_target_pairs={{28,0},{0,4},{4,8},{8,12},{12,16},{16,20},{20,24},{24,28},{29,1},{... | collective-permute-start | bytes 3456008 | tf_op jit(solution)/shard_map/ppermute | solution.py:63
  271.3 2.7 copy-start.14
  282.3 2.7 copy-start.15
  (18 other events, 25.9 us)
Sparse Core Ops, SparseCore 0:
  9.7 54.6 all-gather.5
  66.0 70.9 all-gather.3

commit v2 on v1

v2 whole, which is shorter than its diff:
```python
import functools

import jax
import jax.numpy as jnp
from jax import lax
from jax.experimental import pallas as pl
from jax.experimental.pallas import tpu as pltpu
from jax.sharding import PartitionSpec as P

TILE = 256


def exchange_kernel(walkers, limit, near_ref, occ_near_ref, far_ref, occ_far_ref, k_ref, out_ref):
    step = pl.program_id(0)

    @pl.when(step == 0)
    def _():
        out_ref[...] = jnp.zeros_like(out_ref)

    rows = occ_near_ref.shape[0]
    kern = k_ref[...].astype(jnp.float32)
    lane = step * TILE + lax.broadcasted_iota(jnp.int32, (8, TILE), 1)
    for w in range(walkers):
        near = jnp.dot(near_ref[w], occ_far_ref[...], preferred_element_type=jnp.float32)
        far = jnp.dot(occ_near_ref[...], far_ref[w], preferred_element_type=jnp.float32)
        term = jnp.sum((kern * near * far).reshape(rows // 8, 8, TILE), axis=0)
        out_ref[w] += jnp.where(lane < limit, term, 0.0)


def exchange_block(low, theta, occupied, far, occ_far, k_block):
    walkers, rows, elec = theta.shape
    points = far.shape[2]
    skip = low // TILE
    out = pl.pallas_call(
        functools.partial(exchange_kernel, walkers, points),
        out_shape=jax.ShapeDtypeStruct((walkers, 8, TILE), jnp.float32),
        grid=(pl.cdiv(points, TILE),),
        in_specs=[
            pl.BlockSpec((walkers, rows, elec), lambda j: (0, 0, 0)),
            pl.BlockSpec((rows, elec), lambda j: (0, 0)),
            pl.BlockSpec((walkers, elec, TILE), lambda j: (0, 0, j)),
            pl.BlockSpec((elec, TILE), lambda j: (0, skip + j)),
            pl.BlockSpec((rows, TILE), lambda j: (0, skip + j)),
        ],
        out_specs=pl.BlockSpec((walkers, 8, TILE), lambda j: (0, 0, 0)),
        compiler_params=pltpu.CompilerParams(vmem_limit_bytes=60 * 1024 * 1024),
        cost_estimate=pl.CostEstimate(
            flops=2 * walkers * 2 * rows * points * elec * 2,
            bytes_accessed=2 * rows * points,
            transcendentals=0,
        ),
        name="exchange",
    )(theta, occupied, far, occ_far, k_block)
    return jnp.sum(out, axis=(1, 2))


def shifted(block, distance):
    devices = lax.axis_size("pts")
    return lax.ppermute(block, "pts", [((i - distance) % devices, i) for i in range(devices)])


def local(green_half, collocation, occupied, kernel):
    rows, elec = occupied.shape
    devices = lax.axis_size("pts")
    position = lax.axis_index("pts")
    cut = pl.cdiv(pl.cdiv(rows, TILE), 2) * TILE
    spans = ((0, cut), (cut, rows))
    far_counts = range(1, devices // 2 + 1)

    occ_turned = occupied.T
    occ_far = {}
    travel = occ_turned
    for stride in far_counts:
        travel = shifted(travel, 1)
        occ_far[stride] = travel
    k_blocks = [
        lax.dynamic_slice_in_dim(kernel, ((position - stride) % devices) * rows, rows, 1)
        for stride in range(devices // 2 + 1)
    ]

    parts = []
    for low, high in spans:
        gathered = lax.all_gather(collocation[:, low:high], "wlk", axis=0, tiled=True)
        if low == 0:
            gathered, *k_blocks = lax.optimization_barrier((gathered, *k_blocks))
        parts.append(
            jnp.einsum("wim,mp->wip", green_half, gathered, preferred_element_type=jnp.float32).astype(
                jnp.bfloat16
            )
        )
    theta_turned = jnp.concatenate(parts, axis=2)
    theta = theta_turned.transpose(0, 2, 1)

    far_parts = [{}, {}]
    for h in range(2):
        travel = parts[h]
        for stride in far_counts:
            travel = shifted(travel, 1)
            far_parts[h][stride] = travel

    density = jnp.sum(
        theta_turned.astype(jnp.float32) * occ_turned.astype(jnp.float32)[None], axis=1
    )
    density_b = density.astype(jnp.bfloat16)
    density_all = lax.all_gather(density_b, "pts", axis=1, tiled=True)
    potential = jnp.einsum("wq,aq->wa", density_all, kernel, preferred_element_type=jnp.float32)

    exchange_sum = exchange_block(0, theta, occupied, theta_turned, occ_turned, k_blocks[0])
    for h, (low, high) in enumerate(spans):
        for stride in far_counts:
            weight = 1.0 if 2 * stride == devices else 2.0
            exchange_sum = exchange_sum + weight * exchange_block(
                low, theta, occupied, far_parts[h][stride], occ_far[stride], k_blocks[stride]
            )
    coulomb = 0.5 * jnp.sum(density * potential, axis=1)
    coulomb_energy, exchange_energy = lax.psum((coulomb, -0.5 * exchange_sum), "pts")
    return (potential, coulomb_energy, exchange_energy)


def solution(mesh):
    placed = (P("wlk", None, None), P("wlk", "pts"), P("pts", None), P("pts", None))
    return jax.shard_map(
        local,
        mesh=mesh,
        in_specs=placed,
        out_specs=(P("wlk", "pts"), P("wlk"), P("wlk")),
        check_vma=False,
    )
```

time: 329 us -> 270 us (0.82)
  local copies, waits for them, and re-layouts: 133 us -> 37.7 us
  waiting for transfers between devices: 68.8 us -> 88.2 us
  Pallas kernels: 47.8 us -> 65 us
  blocking collectives: 31.8 us -> 23.7 us
  other arithmetic: 3.74 us -> 11.1 us
    reshape x2 -> x0, local copies, waits for them, and re-layouts: 72 us -> none  [local(): kernel.reshape(rows, kernel.shape[1] // width, width).transpose(1, 0, 2)]
    all_gather x2, waiting for transfers between devices: 23.1 us -> 57.1 us  [local(): lax.all_gather(collocation[:, low:high], 'wlk', axis=0, tiled=True)]
    unnamed x67 -> x22, local copies, waits for them, and re-layouts: 31.4 us -> 8.26 us
    pallas_call x9, Pallas kernels: 47.8 us -> 65 us  [exchange_block(): pl.pallas_call(functools.partial(exchange_kernel, walkers, points), out_s...]
    ppermute x8 -> x0, local copies, waits for them, and re-layouts: 17 us -> none  [shifted(): lax.ppermute(block, 'pts', [((i - distance) % devices, i) for i in range(...]
    dynamic_slice x0 -> x1, local copies, waits for them, and re-layouts: none -> 15.3 us  [local(): lax.dynamic_slice_in_dim(kernel, (position - stride) % devices * rows, ro...]
    ppermute x12, waiting for transfers between devices: 45.7 us -> 31.1 us  [shifted(): lax.ppermute(block, 'pts', [((i - distance) % devices, i) for i in range(...]
    all_gather x1, blocking collectives: 16.9 us -> 9.12 us  [local(): density_all = lax.all_gather(density_b, 'pts', axis=1, tiled=True)]
  transfers between devices with their start and end apart: 14 -> 14, of which waited for: 6 -> 5; matrix products, arithmetic and copies ran while one was open for 42% -> 25% of each run, Pallas kernels for 13% -> 21%
where the time goes in v2:
time: 270 us; the launch traced here: 269 us
  waiting for transfers between devices  88.2 us (33%)
  Pallas kernels  65 us (24%)
  local copies, waits for them, and re-layouts  37.7 us (14%)
  matrix products  24.4 us (9%)
  blocking collectives  23.7 us (9%)
  between operations  14.2 us (5%)
  other arithmetic  11.1 us (4%)
  starting transfers between devices  4.76 us (2%)
    pallas_call x9, Pallas kernels, exchange_block(): pl.pallas_call(functools.partial(exchange_kernel, walkers, points), out_s...  65 us
    all_gather x2, waiting for transfers between devices, local(): lax.all_gather(collocation[:, low:high], 'wlk', axis=0, tiled=True)  57.1 us
    ppermute x12, waiting for transfers between devices, shifted(): lax.ppermute(block, 'pts', [((i - distance) % devices, i) for i in range(...  31.1 us
    dynamic_slice x1, local copies, waits for them, and re-layouts, local(): lax.dynamic_slice_in_dim(kernel, (position - stride) % devices * rows, ro...  15.3 us
    psum x1, blocking collectives, local(): lax.psum((coulomb, -0.5 * exchange_sum), 'pts')  14.6 us
    dot_general x2, matrix products, local(): jnp.einsum('wim,mp->wip', green_half, gathered, preferred_element_type=jn...  13 us
    dot_general x1, matrix products, local(): jnp.einsum('wq,aq->wa', density_all, kernel, preferred_element_type=jnp.f...  11.4 us
    all_gather x1, blocking collectives, local(): density_all = lax.all_gather(density_b, 'pts', axis=1, tiled=True)  9.12 us
  transfers between devices with their start and end apart: 14, of which 5 were waited for; matrix products, arithmetic and copies ran while one was open for 25% of the time, Pallas kernels for 21%

profile of v2, /device:TPU:0, one launch (start us, length us, event | category | flops | bytes accessed | tf_op | source)
XLA Modules:
  0.0 269.2 jit_solution(4091084247043636954)
XLA Ops:
  11.2 48.8 %all-gather.7.cloned.1.call-done = bf16[4,600,432]{1,2,0:T(8,128)(2,1)} async-done(((bf16[1,600,432]{1,2,0:T(8,128)(2,1)}), bf16[4,600,432]{1,2,0:T(8,128)(2,1)}) %all-gather.7.cloned.1.call-update) | async-done | bytes 2073616 | tf_op jit(solution)/shard_map/all_gather | solution.py:83
  60.0 2.5 copy.63
  62.5 2.7 %reshape.12 = bf16[2400,432,1]{0,1,2:T(8,128)(2,1)} reshape(bf16[4,600,432]{1,0,2:T(4,128)(2,1)S(1)} %copy.63) | data formatting | bytes 4147200
  65.2 5.4 %convolution_convert_fusion = bf16[2,400,432]{2,1,0:T(8,128)(2,1)S(1)} fusion(bf16[2,400,2400]{2,1,0:T(8,128)(2,1)} %param.4, bf16[2400,432,1]{0,1,2:T(8,128)(2,1)} %reshape.12), kind=kOutput, calls=%fused_computation.5 | convolution fusion | flops 1659225600 | bytes 6604800 | tf_op jit(solution)/shard_map/wim,mp->wip/dot_general | solution.py:87
  72.2 11.2 %collective-permute-done.8.far_ref = bf16[2,400,432]{2,1,0:T(8,128)(2,1)S(1)} collective-permute-done((bf16[2,400,432]{2,1,0:T(8,128)(2,1)S(1)}, bf16[2,400,432]{2,1,0:T(8,128)(2,1)S(1)}, u32[]{:S(2)}, u32[]{:S(2)}) %collective-permute-start.8) | collective-permute-done | bytes 691232 | tf_op jit(solution)/shard_map/ppermute | solution.py:59
  83.4 11.1 %collective-permute-done.3.occ_far_ref = bf16[400,1200]{1,0:T(8,128)(2,1)} collective-permute-done((bf16[400,1200]{1,0:T(8,128)(2,1)}, bf16[400,1200]{1,0:T(8,128)(2,1)}, u32[]{:S(2)}, u32[]{:S(2)}) %collective-permute-start.3) | collective-permute-done | bytes 960032 | tf_op jit(solution)/shard_map/ppermute | solution.py:59
  94.5 8.8 %collective-permute-done.9.far_ref = bf16[2,400,432]{2,1,0:T(8,128)(2,1)} collective-permute-done((bf16[2,400,432]{2,1,0:T(8,128)(2,1)S(1)}, bf16[2,400,432]{2,1,0:T(8,128)(2,1)}, u32[]{:S(2)}, u32[]{:S(2)}) %collective-permute-start.9) | collective-permute-done | bytes 691232 | tf_op jit(solution)/shard_map/ppermute | solution.py:59
  103.2 15.3 %constant_dynamic-slice_fusion = (bf16[1200,1200]{1,0:T(8,128)(2,1)}, bf16[1200,1200]{1,0:T(8,128)(2,1)}, bf16[1200,1200]{1,0:T(8,128)(2,1)}, bf16[1200,1200]{1,0:T(8,128)(2,1)}, bf16[1200,1200]{1,0:T(8,128)(2,1)}) fusion(bf16[1200,9600]{1,0:T(8,128)(2,1)} %param.7, s32[]{:T(128)S(6)} %select_n.47, s32[]{:T(128)S(6)} %select_n.45, s32[]{:T(128)S(6)} %select_n.43, ...), kind=kLoop, calls=%fused_computation.8 | loop fusion | bytes 28800020 | tf_op jit(solution)/shard_map/dynamic_slice | solution.py:77
  124.4 8.3 %all-gather.5.cloned.1.call-done = bf16[2400,768]{1,0:T(8,128)(2,1)} async-done(((bf16[600,768]{1,0:T(8,128)(2,1)}), bf16[2400,768]{1,0:T(8,128)(2,1)}) %all-gather.5.cloned.1.call-update) | async-done | bytes 3686416 | tf_op jit(solution)/shard_map/all_gather | solution.py:83
  132.8 7.6 %fusion.2 = bf16[768,2,400]{0,2,1:T(8,128)(2,1)} fusion(bf16[2,400,2400]{2,1,0:T(8,128)(2,1)} %param.4, bf16[2400,768]{1,0:T(8,128)(2,1)} %all-gather.5.cloned.1.call-done), kind=kOutput, calls=%fused_computation.4 | convolution fusion | flops 2949734400 | bytes 8755200 | tf_op jit(solution)/shard_map/wim,mp->wip/dot_general | solution.py:87
  142.1 2.7 pad_maximum_fusion
  144.8 4.3 %copy.68.far_ref = bf16[2,400,1200]{2,1,0:T(8,128)(2,1)} copy(bf16[2,400,1200]{1,2,0:T(8,128)(2,1)} %get-tuple-element.22) | data formatting | bytes 3840000 | tf_op jit(solution)/shard_map/concatenate | solution.py:91
  149.1 6.1 %exchange.14 = f32[2,8,256]{2,1,0:T(8,128)} custom-call(bf16[2,1200,400]{2,1,0:T(8,128)(2,1)} %get-tuple-element.23.near_ref, bf16[1200,400]{1,0:T(8,128)(2,1)} %copy.67.occ_near_ref, bf16[2,400,432]{2,1,0:T(8,128)(2,1)} %copy-done.7, bf16[400,1200]{1,0:T(8,128)(2,1)} %collective-permute-done.1.occ_far_ref, bf16[1200,1200]{1,0:T(8,128)(2,1)} %get-tuple-element.11.k_ref), custom_call_target="tpu_custom_call" | custom-call | flops 3317760000 | bytes 1036800 | tf_op jit(solution)/shard_map/exchange/pallas_call | solution.py:34
  155.2 10.5 %exchange.9 = f32[2,8,256]{2,1,0:T(8,128)} custom-call(bf16[2,1200,400]{2,1,0:T(8,128)(2,1)} %get-tuple-element.23.near_ref, bf16[1200,400]{1,0:T(8,128)(2,1)} %copy.67.occ_near_ref, bf16[2,400,1200]{2,1,0:T(8,128)(2,1)} %copy.68.far_ref, bf16[400,1200]{1,0:T(8,128)(2,1)} %bitcast.27, bf16[1200,1200]{1,0:T(8,128)(2,1)} %get-tuple-element.10.k_ref), custom_call_target="tpu_custom_call" | custom-call | flops 9216000000 | bytes 2880000 | tf_op jit(solution)/shard_map/exchange/pallas_call | solution.py:34
  167.3 6.1 %exchange.15 = f32[2,8,256]{2,1,0:T(8,128)} custom-call(bf16[2,1200,400]{2,1,0:T(8,128)(2,1)} %get-tuple-element.23.near_ref, bf16[1200,400]{1,0:T(8,128)(2,1)} %copy.67.occ_near_ref, bf16[2,400,432]{2,1,0:T(8,128)(2,1)} %collective-permute-done.9.far_ref, bf16[400,1200]{1,0:T(8,128)(2,1)} %collective-permute-done.3.occ_far_ref, ...), custom_call_target="tpu_custom_call" | custom-call | flops 3317760000 | bytes 1036800 | tf_op jit(solution)/shard_map/exchange/pallas_call | solution.py:34
  174.4 6.1 %exchange.16 = f32[2,8,256]{2,1,0:T(8,128)} custom-call(bf16[2,1200,400]{2,1,0:T(8,128)(2,1)} %get-tuple-element.23.near_ref, bf16[1200,400]{1,0:T(8,128)(2,1)} %copy.67.occ_near_ref, bf16[2,400,432]{2,1,0:T(8,128)(2,1)} %collective-permute-done.10.far_ref, bf16[400,1200]{1,0:T(8,128)(2,1)} %collective-permute-done.5.occ_far_ref, ...), custom_call_target="tpu_custom_call" | custom-call | flops 3317760000 | bytes 1036800 | tf_op jit(solution)/shard_map/exchange/pallas_call | solution.py:34
  183.6 9.1 %all-gather.1 = bf16[8,1200,2]{1,2,0:T(2,128)(2,1)S(1)} all-gather(bf16[1,1200,2]{1,2,0:T(2,128)(2,1)S(1)} %convert_bitcast_fusion), channel_id=1, replica_groups=mesh['pts'=8,'wlk'=4] {'pts'}, dimensions={0}, use_global_device_ids=true | all-gather | bytes 43200 | tf_op jit(solution)/shard_map/all_gather | solution.py:105
  193.6 11.4 %multiply_reduce_fusion.1 = (f32[2]{0:T(128)S(1)}, f32[2,1200]{1,0:T(2,128)}) fusion(f32[2,1200]{1,0:T(2,128)S(1)} %multiply_reduce_fusion, bf16[9600,2]{0,1:T(2,128)(2,1)S(1)} %reshape.10, bf16[1200,9600]{1,0:T(8,128)(2,1)} %param.7), kind=kOutput, calls=%fused_computation.6 | convolution fusion | flops 46084800 | bytes 23097608 | tf_op jit(solution)/shard_map/wq,aq->wa/dot_general | solution.py:106
  205.9 6.1 %exchange.17 = f32[2,8,256]{2,1,0:T(8,128)} custom-call(bf16[2,1200,400]{2,1,0:T(8,128)(2,1)} %get-tuple-element.23.near_ref, bf16[1200,400]{1,0:T(8,128)(2,1)} %copy.67.occ_near_ref, bf16[2,400,432]{2,1,0:T(8,128)(2,1)} %copy-done.8, bf16[400,1200]{1,0:T(8,128)(2,1)} %collective-permute-done.7.occ_far_ref, bf16[1200,1200]{1,0:T(8,128)(2,1)} %get-tuple-element.14.k_ref), custom_call_target="tpu_custom_call" | custom-call | flops 3317760000 | bytes 1036800 | tf_op jit(solution)/shard_map/exchange/pallas_call | solution.py:34
  213.1 7.6 %exchange.10 = f32[2,8,256]{2,1,0:T(8,128)} custom-call(bf16[2,1200,400]{2,1,0:T(8,128)(2,1)} %get-tuple-element.23.near_ref, bf16[1200,400]{1,0:T(8,128)(2,1)} %copy.67.occ_near_ref, bf16[2,400,768]{2,1,0:T(8,128)(2,1)} %collective-permute-done.far_ref, bf16[400,1200]{1,0:T(8,128)(2,1)} %collective-permute-done.1.occ_far_ref, ...), custom_call_target="tpu_custom_call" | custom-call | flops 5898240000 | bytes 1843200 | tf_op jit(solution)/shard_map/exchange/pallas_call | solution.py:34
  221.6 7.6 %exchange.11 = f32[2,8,256]{2,1,0:T(8,128)} custom-call(bf16[2,1200,400]{2,1,0:T(8,128)(2,1)} %get-tuple-element.23.near_ref, bf16[1200,400]{1,0:T(8,128)(2,1)} %copy.67.occ_near_ref, bf16[2,400,768]{2,1,0:T(8,128)(2,1)} %collective-permute-done.2.far_ref, bf16[400,1200]{1,0:T(8,128)(2,1)} %collective-permute-done.3.occ_far_ref, ...), custom_call_target="tpu_custom_call" | custom-call | flops 5898240000 | bytes 1843200 | tf_op jit(solution)/shard_map/exchange/pallas_call | solution.py:34
  229.9 7.6 %exchange.12 = f32[2,8,256]{2,1,0:T(8,128)} custom-call(bf16[2,1200,400]{2,1,0:T(8,128)(2,1)} %get-tuple-element.23.near_ref, bf16[1200,400]{1,0:T(8,128)(2,1)} %copy.67.occ_near_ref, bf16[2,400,768]{2,1,0:T(8,128)(2,1)} %copy-done.5, bf16[400,1200]{1,0:T(8,128)(2,1)} %collective-permute-done.5.occ_far_ref, bf16[1200,1200]{1,0:T(8,128)(2,1)} %get-tuple-element.13.k_ref), custom_call_target="tpu_custom_call" | custom-call | flops 5898240000 | bytes 1843200 | tf_op jit(solution)/shard_map/exchange/pallas_call | solution.py:34
  239.4 7.6 %exchange.13 = f32[2,8,256]{2,1,0:T(8,128)} custom-call(bf16[2,1200,400]{2,1,0:T(8,128)(2,1)} %get-tuple-element.23.near_ref, bf16[1200,400]{1,0:T(8,128)(2,1)} %copy.67.occ_near_ref, bf16[2,400,768]{2,1,0:T(8,128)(2,1)} %copy-done.6, bf16[400,1200]{1,0:T(8,128)(2,1)} %collective-permute-done.7.occ_far_ref, bf16[1200,1200]{1,0:T(8,128)(2,1)} %get-tuple-element.14.k_ref), custom_call_target="tpu_custom_call" | custom-call | flops 5898240000 | bytes 1843200 | tf_op jit(solution)/shard_map/exchange/pallas_call | solution.py:34
  247.8 14.6 %all-reduce = (f32[2]{0:T(128)}, f32[2]{0:T(128)}) all-reduce(f32[2]{0:T(128)S(1)} %get-tuple-element.27, f32[2]{0:T(128)S(1)} %get-tuple-element.26), channel_id=1, replica_groups=mesh['pts'=8,'wlk'=4] {'pts'}, use_global_device_ids=true, to_apply=%region_2.3 | all-reduce | flops 4 | bytes 32 | tf_op jit(solution)/shard_map/psum | solution.py:116
  (65 shorter events, 26.2 us)
Async XLA Ops:
  7.2 2.5 copy-start.1
  7.2 3.5 %copy-start = (bf16[1200,400]{0,1:T(8,128)(2,1)S(1)}, bf16[1200,400]{0,1:T(8,128)(2,1)}, u32[]{:S(2)}) copy-start(bf16[1200,400]{0,1:T(8,128)(2,1)} %param.6) | copy-start | bytes 2880004
  7.2 52.8 %all-gather.7.cloned.1.call-start = ((), (), s32[]{:S(2)}) async-start(), calls=%async_computation.1 | async-start | bytes 2764800 | tf_op jit(solution)/shard_map/all_gather | solution.py:83
  9.6 123.2 %all-gather.5.cloned.1.call-start = ((), (), s32[]{:S(2)}) async-start(), calls=%async_computation | async-start | bytes 4608000 | tf_op jit(solution)/shard_map/all_gather | solution.py:83
  10.7 60.1 %collective-permute-start.1 = (bf16[400,1200]{1,0:T(8,128)(2,1)S(1)}, bf16[400,1200]{1,0:T(8,128)(2,1)}, u32[]{:S(2)}, u32[]{:S(2)}) collective-permute-start(bf16[400,1200]{1,0:T(8,128)(2,1)S(1)} %bitcast.28), channel_id=1, source_target_pairs={{28,0},{0,4},{4,8},{8,12},{12,16},{16,20},{20,24},{24,28},{29,1},{... | collective-permute-start | bytes 2880008 | tf_op jit(solution)/shard_map/ppermute | solution.py:59
  70.7 0.9 copy-start.2
  70.7 12.7 %collective-permute-start.8 = (bf16[2,400,432]{2,1,0:T(8,128)(2,1)S(1)}, bf16[2,400,432]{2,1,0:T(8,128)(2,1)S(1)}, u32[]{:S(2)}, u32[]{:S(2)}) collective-permute-start(bf16[2,400,432]{2,1,0:T(8,128)(2,1)S(1)} %convolution_convert_fusion), channel_id=1, source_target_pairs={{28,0},{0,4},{4,8},{8,12},{12,16},{16,20},{20,24},{24,28},{29,1},{... | collective-permute-start | bytes 2073608 | tf_op jit(solution)/shard_map/ppermute | solution.py:59
  71.6 22.9 %collective-permute-start.3 = (bf16[400,1200]{1,0:T(8,128)(2,1)}, bf16[400,1200]{1,0:T(8,128)(2,1)}, u32[]{:S(2)}, u32[]{:S(2)}) collective-permute-start(bf16[400,1200]{1,0:T(8,128)(2,1)} %collective-permute-done.1.occ_far_ref), channel_id=1, source_target_pairs={{28,0},{0,4},{4,8},{8,12},{12,16},{16,20},{20,24},{24,28},{29,1},{... | collective-permute-start | bytes 2880008 | tf_op jit(solution)/shard_map/ppermute | solution.py:59
  83.4 35.1 %copy-start.7 = (bf16[2,400,432]{2,1,0:T(8,128)(2,1)}, bf16[2,400,432]{2,1,0:T(8,128)(2,1)S(1)}, u32[]{:S(2)}) copy-start(bf16[2,400,432]{2,1,0:T(8,128)(2,1)S(1)} %collective-permute-done.8.far_ref) | copy-start | bytes 2073604
  83.4 19.9 %collective-permute-start.9 = (bf16[2,400,432]{2,1,0:T(8,128)(2,1)S(1)}, bf16[2,400,432]{2,1,0:T(8,128)(2,1)}, u32[]{:S(2)}, u32[]{:S(2)}) collective-permute-start(bf16[2,400,432]{2,1,0:T(8,128)(2,1)S(1)} %collective-permute-done.8.far_ref), channel_id=1, source_target_pairs={{28,0},{0,4},{4,8},{8,12},{12,16},{16,20},{20,24},{24,28},{29,1},{... | collective-permute-start | bytes 2073608 | tf_op jit(solution)/shard_map/ppermute | solution.py:59
  94.5 27.8 %collective-permute-start.5 = (bf16[400,1200]{1,0:T(8,128)(2,1)}, bf16[400,1200]{1,0:T(8,128)(2,1)}, u32[]{:S(2)}, u32[]{:S(2)}) collective-permute-start(bf16[400,1200]{1,0:T(8,128)(2,1)} %collective-permute-done.3.occ_far_ref), channel_id=1, source_target_pairs={{28,0},{0,4},{4,8},{8,12},{12,16},{16,20},{20,24},{24,28},{29,1},{... | collective-permute-start | bytes 2880008 | tf_op jit(solution)/shard_map/ppermute | solution.py:59
  103.2 20.9 %collective-permute-start.10 = (bf16[2,400,432]{2,1,0:T(8,128)(2,1)}, bf16[2,400,432]{2,1,0:T(8,128)(2,1)}, u32[]{:S(2)}, u32[]{:S(2)}) collective-permute-start(bf16[2,400,432]{2,1,0:T(8,128)(2,1)} %collective-permute-done.9.far_ref), channel_id=1, source_target_pairs={{28,0},{0,4},{4,8},{8,12},{12,16},{16,20},{20,24},{24,28},{29,1},{... | collective-permute-start | bytes 2073608 | tf_op jit(solution)/shard_map/ppermute | solution.py:59
  122.3 82.7 %collective-permute-start.7 = (bf16[400,1200]{1,0:T(8,128)(2,1)}, bf16[400,1200]{1,0:T(8,128)(2,1)}, u32[]{:S(2)}, u32[]{:S(2)}) collective-permute-start(bf16[400,1200]{1,0:T(8,128)(2,1)} %collective-permute-done.5.occ_far_ref), channel_id=1, source_target_pairs={{28,0},{0,4},{4,8},{8,12},{12,16},{16,20},{20,24},{24,28},{29,1},{... | collective-permute-start | bytes 2880008 | tf_op jit(solution)/shard_map/ppermute | solution.py:59
  124.2 80.8 %collective-permute-start.11 = (bf16[2,400,432]{2,1,0:T(8,128)(2,1)}, bf16[2,400,432]{2,1,0:T(8,128)(2,1)S(1)}, u32[]{:S(2)}, u32[]{:S(2)}) collective-permute-start(bf16[2,400,432]{2,1,0:T(8,128)(2,1)} %collective-permute-done.10.far_ref), channel_id=1, source_target_pairs={{28,0},{0,4},{4,8},{8,12},{12,16},{16,20},{20,24},{24,28},{29,1},{... | collective-permute-start | bytes 2073608 | tf_op jit(solution)/shard_map/ppermute | solution.py:59
  142.0 23.6 %collective-permute-start = (bf16[2,400,768]{2,1,0:T(8,128)(2,1)}, bf16[2,400,768]{2,1,0:T(8,128)(2,1)}, u32[]{:S(2)}, u32[]{:S(2)}) collective-permute-start(bf16[2,400,768]{2,1,0:T(8,128)(2,1)} %bitcast.30), channel_id=1, source_target_pairs={{28,0},{0,4},{4,8},{8,12},{12,16},{16,20},{20,24},{24,28},{29,1},{... | collective-permute-start | bytes 3686408 | tf_op jit(solution)/shard_map/ppermute | solution.py:59
  165.7 7.7 %copy-start.4 = (f32[2,8,256]{2,1,0:T(8,128)S(1)}, f32[2,8,256]{2,1,0:T(8,128)}, u32[]{:S(2)}) copy-start(f32[2,8,256]{2,1,0:T(8,128)} %exchange.9) | copy-start | bytes 49156
  165.7 7.8 %copy-start.3 = (f32[2,8,256]{2,1,0:T(8,128)S(1)}, f32[2,8,256]{2,1,0:T(8,128)}, u32[]{:S(2)}) copy-start(f32[2,8,256]{2,1,0:T(8,128)} %exchange.14) | copy-start | bytes 49156
  165.7 27.3 %collective-permute-start.2 = (bf16[2,400,768]{2,1,0:T(8,128)(2,1)}, bf16[2,400,768]{2,1,0:T(8,128)(2,1)}, u32[]{:S(2)}, u32[]{:S(2)}) collective-permute-start(bf16[2,400,768]{2,1,0:T(8,128)(2,1)} %collective-permute-done.far_ref), channel_id=1, source_target_pairs={{28,0},{0,4},{4,8},{8,12},{12,16},{16,20},{20,24},{24,28},{29,1},{... | collective-permute-start | bytes 3686408 | tf_op jit(solution)/shard_map/ppermute | solution.py:59
  192.9 19.8 %collective-permute-start.4 = (bf16[2,400,768]{2,1,0:T(8,128)(2,1)}, bf16[2,400,768]{2,1,0:T(8,128)(2,1)S(1)}, u32[]{:S(2)}, u32[]{:S(2)}) collective-permute-start(bf16[2,400,768]{2,1,0:T(8,128)(2,1)} %collective-permute-done.2.far_ref), channel_id=1, source_target_pairs={{28,0},{0,4},{4,8},{8,12},{12,16},{16,20},{20,24},{24,28},{29,1},{... | collective-permute-start | bytes 3686408 | tf_op jit(solution)/shard_map/ppermute | solution.py:59
  205.0 0.9 copy-start.8
  212.7 8.0 %copy-start.5 = (bf16[2,400,768]{2,1,0:T(8,128)(2,1)}, bf16[2,400,768]{2,1,0:T(8,128)(2,1)S(1)}, u32[]{:S(2)}) copy-start(bf16[2,400,768]{2,1,0:T(8,128)(2,1)S(1)} %collective-permute-done.4.far_ref) | copy-start | bytes 3686404
  212.7 25.6 %collective-permute-start.6 = (bf16[2,400,768]{2,1,0:T(8,128)(2,1)S(1)}, bf16[2,400,768]{2,1,0:T(8,128)(2,1)S(1)}, u32[]{:S(2)}, u32[]{:S(2)}) collective-permute-start(bf16[2,400,768]{2,1,0:T(8,128)(2,1)S(1)} %collective-permute-done.4.far_ref), channel_id=1, source_target_pairs={{28,0},{0,4},{4,8},{8,12},{12,16},{16,20},{20,24},{24,28},{29,1},{... | collective-permute-start | bytes 3686408 | tf_op jit(solution)/shard_map/ppermute | solution.py:59
  238.3 1.0 copy-start.6
Sparse Core Ops, SparseCore 0:
  9.7 50.2 all-gather.6
  61.6 71.1 all-gather.4
